TPU v7x, 32 devices: a whole 2x2x4 slice. The times are simulated.
32 devices in a mesh: rep: 2 (over y), tp: 4 (over z), ep: 4 (over x, core).
Axes of the slice: x: 2, y: 2, z: 4, core: 2. Of those that a mesh axis runs over, the one named last changes fastest.
Arguments:
- tokens: bfloat16 [768, 3072], P(('rep', 'ep'), 'tp'), parts along dimension 0, may hold values from -6 to 6
- routing: int32 [768, 2], P(('rep', 'ep')), parts along dimension 0, may hold values from 0 to 3, all different within a row; in each aligned block of 96 rows (0 to 95, 96 to 191, ...) at most 54 rows name the same one
- route_gates: float32 [768, 2], P(('rep', 'ep')), parts along dimension 0, may hold values from 0.2 to 1
- expert_gate: bfloat16 [4, 3072, 8192], P('ep', None, 'tp'), may hold values from -0.109375 to 0.109375
- expert_up: bfloat16 [4, 3072, 8192], P('ep', None, 'tp'), may hold values from -0.109375 to 0.109375
- expert_down: bfloat16 [4, 8192, 3072], P('ep', 'tp'), may hold values from -0.0625 to 0.0625
Outputs:
- mixture: bfloat16 [768, 3072], P(('rep', 'ep'), 'tp'), parts along dimension 0
There are 2 independent parts, one for each index of `rep`. A program takes and returns all parts, laid end to end along the dimension named above; an argument that names none is the same for every part. Nothing has to cross between parts.
Inputs may be any that keep to these rules, and one draw needn't show every extreme that they name: `routing`: each token names two different experts. In each aligned block of 96 tokens (the rows of one index of ep) no expert is named by more than 54 tokens, a bound that some block reaches.
All inputs are finite; a program needn't handle non-finite values.
Results may differ from a plain program's by a relative error of at most 0.0085.
Values may be sent and summed in bfloat16 or wider, within the bound.
A program may use at most 128 MiB of HBM per device.

v0:
```python
import jax
import jax.numpy as jnp
from jax import lax
from jax.sharding import PartitionSpec as P


def slot_tables(routing, route_gates, experts, capacity):
    count_rows = routing.shape[0]
    choices_n = routing.shape[1]
    flat_ids = routing.reshape(-1)
    onehot = (flat_ids[:, None] == jnp.arange(experts, dtype=jnp.int32)[None, :]).astype(jnp.int32)
    before = jnp.cumsum(onehot, axis=0) - onehot
    position = jnp.sum(before * onehot, axis=1)
    slot_index = flat_ids * capacity + position
    picked = (
        slot_index[:, None] == jnp.arange(experts * capacity, dtype=jnp.int32)[None, :]
    ).astype(jnp.float32)
    dispatch = picked.reshape(count_rows, choices_n, experts * capacity).sum(axis=1)
    combine = (
        (picked * route_gates.reshape(-1)[:, None])
        .reshape(count_rows, choices_n, experts * capacity)
        .sum(axis=1)
    )
    return (dispatch, combine)


def hidden_rows(everyone, expert_gate, expert_up, capacity):
    local_count = expert_gate.shape[0]
    total = everyone.shape[0]
    row_block = everyone.reshape(
        total // (local_count * capacity), local_count, capacity, everyone.shape[1]
    )
    gate_part = jnp.einsum(
        "tlcd,ldf->tlcf", row_block, expert_gate, preferred_element_type=jnp.float32
    )
    upward = jnp.einsum("tlcd,ldf->tlcf", row_block, expert_up, preferred_element_type=jnp.float32)
    return (jax.nn.silu(gate_part) * upward).astype(jnp.bfloat16)


def body(tokens, routing, route_gates, expert_gate, expert_up, expert_down):
    local_count = expert_gate.shape[0]
    ep_count = lax.axis_size("ep")
    tp_count = lax.axis_size("tp")
    tok_count = tokens.shape[0]
    capacity = 2 * tok_count // ep_count + tok_count // 16
    experts = local_count * ep_count
    dispatch, combine = slot_tables(routing, route_gates, experts, capacity)
    dispatch_low = dispatch.astype(jnp.bfloat16)
    whole = lax.all_gather(tokens, "tp", axis=1, tiled=True)
    packed = jnp.einsum(
        "tc,td->cd", dispatch_low, whole, preferred_element_type=jnp.float32
    ).astype(jnp.bfloat16)
    everyone = lax.all_to_all(packed, "ep", split_axis=0, concat_axis=0, tiled=True)
    total_rows = everyone.shape[0]
    columns = everyone.shape[1]
    hidden = hidden_rows(everyone, expert_gate, expert_up, capacity)
    part = jnp.einsum("tlcf,lfd->dtlc", hidden, expert_down, preferred_element_type=jnp.float32)
    summed_t = lax.psum_scatter(
        part.reshape(columns // tp_count * lax.axis_size("tp"), total_rows),
        "tp",
        scatter_dimension=0,
        tiled=True,
    )
    summed = summed_t.T
    expert_out = summed.astype(jnp.bfloat16)
    returned = lax.all_to_all(expert_out, "ep", split_axis=0, concat_axis=0, tiled=True)
    mixed = jnp.dot(combine, returned.astype(jnp.float32), precision=lax.Precision.HIGHEST)
    return mixed.astype(jnp.bfloat16)


def solution(mesh):
    return jax.shard_map(
        body,
        mesh=mesh,
        in_specs=(
            P(("rep", "ep"), "tp"),
            P(("rep", "ep"), None),
            P(("rep", "ep"), None),
            P("ep", None, "tp"),
            P("ep", None, "tp"),
            P("ep", "tp", None),
        ),
        out_specs=P(("rep", "ep"), "tp"),
        check_vma=False,
    )
```

profile of v0, /device:TPU:0, one launch (start us, length us, event | category | flops | bytes accessed | tf_op | source)
XLA Modules:
  0.0 145.9 jit_solution(12279673939200975978)
XLA Ops:
  6.5 0.0 reduce-scatter.2.cloned.1.call-start
  6.5 0.8 copy.23
  7.3 0.1 eq.37
  7.5 1.2 reduce-window.6
  8.7 0.1 slice.12
  8.8 0.1 copy.24
  8.9 0.1 copy.25
  9.0 0.1 add_bitcast_fusion
  9.1 0.1 reduce_sum.30
  9.3 0.1 copy.26
  9.3 0.7 multiply_add_fusion
  10.1 18.5 %all_gather.3 = bf16[96,3072]{1,0:T(8,128)(2,1)S(1)} all-gather(bf16[96,768]{1,0:T(8,128)(2,1)} %param.6), channel_id=1, replica_groups=mesh['rep'=2,'tp'=4,'ep'=4] {'tp'}, dimensions={1}, use_global_device_ids=true | all-gather | bytes 737280 | tf_op jit(solution)/shard_map/all_gather | solution.py:49
  28.5 0.8 convert_reduce_fusion
  29.3 0.5 convolution_convert_fusion
  29.9 0.4 all_to_all.14
  30.2 20.5 %all_to_all.21 = bf16[4,54,3072]{2,1,0:T(8,128)(2,1)S(1)} all-to-all(bf16[4,54,3072]{2,1,0:T(8,128)(2,1)S(1)} %all_to_all.14), channel_id=1, replica_groups=mesh['rep'=2,'tp'=4,'ep'=4] {'ep'}, dimensions={0} | all-to-all | bytes 2654208 | tf_op jit(solution)/shard_map/all_to_all | solution.py:53
  50.7 6.3 %fusion.9 = f32[4,1,54,2048]{3,2,0,1:T(8,128)S(1)} fusion(bf16[4,54,3072]{2,1,0:T(8,128)(2,1)S(1)} %all_to_all.21, bf16[1,3072,2048]{2,1,0:T(8,128)(2,1)} %param.9), kind=kOutput, calls=%fused_computation.8 | convolution fusion | flops 2717908992 | bytes 15679488 | tf_op jit(solution)/shard_map/tlcd,ldf->tlcf/dot_general | solution.py:33
  57.0 7.9 %fusion.18 = bf16[4,1,54,2048]{3,2,0,1:T(8,128)(2,1)S(1)} fusion(bf16[4,54,3072]{2,1,0:T(8,128)(2,1)S(1)} %all_to_all.21, bf16[1,3072,2048]{2,1,0:T(8,128)(2,1)} %param.10, f32[4,1,54,2048]{3,2,0,1:T(8,128)S(1)} %fusion.9), kind=kOutput, calls=%fused_computation.11 | convolution fusion | flops 2720563200 | bytes 16564224 | tf_op jit(solution)/shard_map/tlcd,ldf->tlcf/dot_general | solution.py:36
  64.9 0.2 dot_general.34
  65.1 9.0 %fusion.6 = f32[3072,216]{0,1:T(8,128)} fusion(bf16[216,2048]{1,0:T(8,128)(2,1)S(1)} %dot_general.34, bf16[1,2048,3072]{2,1,0:T(8,128)(2,1)} %param.11), kind=kOutput, calls=%fused_computation.6 | convolution fusion | flops 2717908992 | bytes 16121856 | tf_op jit(solution)/shard_map/tlcf,lfd->dtlc/dot_general | solution.py:57
  74.1 0.0 reduce-scatter.2.cloned.1.call-update
  74.2 53.2 %reduce-scatter.2.cloned.1.call-done = f32[768,216]{0,1:T(8,128)} async-done(((f32[3072,216]{0,1:T(8,128)}), f32[768,216]{0,1:T(8,128)}) %reduce-scatter.2.cloned.1.call-update) | async-done | bytes 663568 | tf_op jit(solution)/shard_map/reduce_scatter | solution.py:58
  127.4 1.1 convert_bitcast_fusion
  128.5 0.1 all_to_all.16
  128.6 9.4 %all_to_all.22 = bf16[4,54,768]{2,1,0:T(8,128)(2,1)S(1)} all-to-all(bf16[4,54,768]{2,1,0:T(8,128)(2,1)S(1)} %all_to_all.16), channel_id=1, replica_groups=mesh['rep'=2,'tp'=4,'ep'=4] {'ep'}, dimensions={0} | all-to-all | bytes 663552 | tf_op jit(solution)/shard_map/all_to_all | solution.py:66
  138.0 0.1 all_to_all.18
  138.1 1.0 convolution_convert_fusion.1
  (7 shorter events, 0.1 us)
Async XLA Ops:
  6.5 120.8 %reduce-scatter.2.cloned.1.call-start = ((), (), s32[]{:S(2)}) async-start(), calls=%async_computation.3 | async-start | bytes 3317760 | tf_op jit(solution)/shard_map/reduce_scatter | solution.py:58
Sparse Core Ops, SparseCore 0:
  74.3 53.0 reduce-scatter.1
where the time goes:
time: 146 us
  waiting for transfers between devices  53.2 us (36%)
  blocking collectives  48.4 us (33%)
  matrix products  24.6 us (17%)
  between operations  13.5 us (9%)
  other arithmetic  4.01 us (3%)
  local copies, waits for them, and re-layouts  2.2 us (2%)
    reduce_scatter x1, waiting for transfers between devices, body(): lax.psum_scatter(part.reshape(columns // tp_count * lax.axis_size('tp'),...  53.2 us
    all_to_all x1, blocking collectives, body(): lax.all_to_all(packed, 'ep', split_axis=0, concat_axis=0, tiled=True)  20.5 us
    all_gather x1, blocking collectives, body(): whole = lax.all_gather(tokens, 'tp', axis=1, tiled=True)  18.5 us
    all_to_all x1, blocking collectives, body(): lax.all_to_all(expert_out, 'ep', split_axis=0, concat_axis=0, tiled=True)  9.41 us
    dot_general x1, matrix products, body(): jnp.einsum('tlcf,lfd->dtlc', hidden, expert_down, preferred_element_type=...  9.01 us
    dot_general x1, matrix products, hidden_rows(): jnp.einsum('tlcd,ldf->tlcf', row_block, expert_up, preferred_element_type...  7.89 us
    dot_general x1, matrix products, hidden_rows(): jnp.einsum('tlcd,ldf->tlcf', row_block, expert_gate, preferred_element_ty...  6.26 us
  transfers between devices with their start and end apart: 1, of which 1 were waited for; matrix products, arithmetic and copies ran while one was open for 0% of the time, Pallas kernels for 0%

commit v1 on v0

--- a/solution.py
+++ b/solution.py
@@ -2,6 +2,21 @@
 import jax.numpy as jnp
 from jax import lax
 from jax.sharding import PartitionSpec as P
+
+
+def work_around(value, axis, dim, make, out_dim):
+    ways, here, lap = (lax.axis_size(axis), lax.axis_index(axis), value.shape[dim])
+    results = []
+    for far in range(ways):
+        arriving = (
+            lax.ppermute(value, axis, [(d, (d + 1) % ways) for d in range(ways)])
+            if far + 1 < ways
+            else value
+        )
+        results.append(make(value, (here - far) % ways * lap))
+        value = arriving
+    line = jnp.concatenate(results[::-1], axis=out_dim)
+    return jnp.roll(line, (here + 1) * results[0].shape[out_dim], axis=out_dim)
 
 
 def slot_tables(routing, route_gates, experts, capacity):
@@ -46,9 +61,14 @@
     experts = local_count * ep_count
     dispatch, combine = slot_tables(routing, route_gates, experts, capacity)
     dispatch_low = dispatch.astype(jnp.bfloat16)
-    whole = lax.all_gather(tokens, "tp", axis=1, tiled=True)
-    packed = jnp.einsum(
-        "tc,td->cd", dispatch_low, whole, preferred_element_type=jnp.float32
+    packed = work_around(
+        tokens,
+        "tp",
+        1,
+        lambda shard, at: jnp.einsum(
+            "tc,td->cd", dispatch_low, shard, preferred_element_type=jnp.float32
+        ),
+        1,
     ).astype(jnp.bfloat16)
     everyone = lax.all_to_all(packed, "ep", split_axis=0, concat_axis=0, tiled=True)
     total_rows = everyone.shape[0]

time: 146 us -> 145 us (level)
  blocking collectives: 48.4 us -> 29.9 us
  waiting for transfers between devices: 53.2 us -> 66 us
  starting transfers between devices: 0.01 us -> 3.06 us
    all_gather x1 -> x0, blocking collectives: 18.5 us -> none  [body(): whole = lax.all_gather(tokens, 'tp', axis=1, tiled=True)]
    ppermute x0 -> x3, waiting for transfers between devices: none -> 15.7 us  [work_around(): lax.ppermute(value, axis, [(d, (d + 1) % ways) for d in range(ways)])]
    ppermute x0 -> x3, starting transfers between devices: none -> 3.06 us  [work_around(): lax.ppermute(value, axis, [(d, (d + 1) % ways) for d in range(ways)])]
    reduce_scatter x1, waiting for transfers between devices: 53.2 us -> 50.2 us  [body(): lax.psum_scatter(part.reshape(columns // tp_count * lax.axis_size('tp'),...]
  transfers between devices with their start and end apart: 1 -> 4, of which waited for: 1 -> 4; matrix products, arithmetic and copies ran while one was open for 0% -> 3% of each run, Pallas kernels for 0% -> 0%
where the time goes in v1:
time: 145 us; the launch traced here: 144 us
  waiting for transfers between devices  66 us (46%)
  blocking collectives  29.9 us (21%)
  matrix products  25.2 us (17%)
  between operations  13.5 us (9%)
  other arithmetic  3.98 us (3%)
  starting transfers between devices  3.06 us (2%)
  local copies, waits for them, and re-layouts  2.84 us (2%)
    reduce_scatter x1, waiting for transfers between devices, body(): lax.psum_scatter(part.reshape(columns // tp_count * lax.axis_size('tp'),...  50.2 us
    all_to_all x1, blocking collectives, body(): lax.all_to_all(packed, 'ep', split_axis=0, concat_axis=0, tiled=True)  20.5 us
    ppermute x3, waiting for transfers between devices, work_around(): lax.ppermute(value, axis, [(d, (d + 1) % ways) for d in range(ways)])  15.7 us
    all_to_all x1, blocking collectives, body(): lax.all_to_all(expert_out, 'ep', split_axis=0, concat_axis=0, tiled=True)  9.41 us
    dot_general x1, matrix products, body(): jnp.einsum('tlcf,lfd->dtlc', hidden, expert_down, preferred_element_type=...  9.01 us
    dot_general x1, matrix products, hidden_rows(): jnp.einsum('tlcd,ldf->tlcf', row_block, expert_up, preferred_element_type...  7.89 us
    dot_general x1, matrix products, hidden_rows(): jnp.einsum('tlcd,ldf->tlcf', row_block, expert_gate, preferred_element_ty...  6.25 us
    ppermute x3, starting transfers between devices, work_around(): lax.ppermute(value, axis, [(d, (d + 1) % ways) for d in range(ways)])  3.06 us
  transfers between devices with their start and end apart: 4, of which 4 were waited for; matrix products, arithmetic and copies ran while one was open for 3% of the time, Pallas kernels for 0%

profile of v1, /device:TPU:0, one launch (start us, length us, event | category | flops | bytes accessed | tf_op | source)
XLA Modules:
  0.0 144.5 jit_solution(7979003311763664559)
XLA Ops:
  6.5 3.1 %collective-permute-start = (bf16[96,768]{1,0:T(8,128)(2,1)}, bf16[96,768]{1,0:T(8,128)(2,1)S(1)}, u32[]{:S(2)}, u32[]{:S(2)}) collective-permute-start(bf16[96,768]{1,0:T(8,128)(2,1)} %param.6), channel_id=1, source_target_pairs={{0,4},{4,8},{8,12},{12,0},{1,5},{5,9},{9,13},{13,1},{2,6},{6,10},{... | collective-permute-start | bytes 442376 | tf_op jit(solution)/shard_map/ppermute | solution.py:12
  9.6 0.8 copy.23
  10.4 0.1 eq.40
  10.5 1.2 reduce-window.6
  11.8 0.1 slice.12
  11.8 0.1 copy.24
  12.0 0.1 copy.25
  12.1 3.7 %collective-permute-done = bf16[96,768]{1,0:T(8,128)(2,1)S(1)} collective-permute-done((bf16[96,768]{1,0:T(8,128)(2,1)}, bf16[96,768]{1,0:T(8,128)(2,1)S(1)}, u32[]{:S(2)}, u32[]{:S(2)}) %collective-permute-start) | collective-permute-done | bytes 147488 | tf_op jit(solution)/shard_map/ppermute | solution.py:12
  15.7 0.1 add_bitcast_fusion
  15.8 0.1 reduce_sum.30
  16.0 0.1 copy.26
  16.1 6.6 %collective-permute-done.1 = bf16[96,768]{1,0:T(8,128)(2,1)S(1)} collective-permute-done((bf16[96,768]{1,0:T(8,128)(2,1)S(1)}, bf16[96,768]{1,0:T(8,128)(2,1)S(1)}, u32[]{:S(2)}, u32[]{:S(2)}) %collective-permute-start.1) | collective-permute-done | bytes 147488 | tf_op jit(solution)/shard_map/ppermute | solution.py:12
  22.7 0.7 multiply_add_fusion
  23.4 0.8 convert_reduce_fusion
  24.2 5.4 %collective-permute-done.2 = bf16[96,768]{1,0:T(8,128)(2,1)S(1)} collective-permute-done((bf16[96,768]{1,0:T(8,128)(2,1)S(1)}, bf16[96,768]{1,0:T(8,128)(2,1)S(1)}, u32[]{:S(2)}, u32[]{:S(2)}) %collective-permute-start.2) | collective-permute-done | bytes 147488 | tf_op jit(solution)/shard_map/ppermute | solution.py:12
  29.6 0.3 constant_dynamic-update-slice_fusion.7
  29.9 0.3 constant_dynamic-update-slice_fusion.6
  30.2 0.3 constant_dynamic-update-slice_fusion.5
  30.5 0.3 constant_dynamic-update-slice_fusion.4
  30.9 0.5 dynamic-slice_convert_fusion
  31.4 0.4 all_to_all.14
  31.8 20.5 %all_to_all.21 = bf16[4,54,3072]{2,1,0:T(8,128)(2,1)S(1)} all-to-all(bf16[4,54,3072]{2,1,0:T(8,128)(2,1)S(1)} %all_to_all.14), channel_id=1, replica_groups=mesh['rep'=2,'tp'=4,'ep'=4] {'ep'}, dimensions={0} | all-to-all | bytes 2654208 | tf_op jit(solution)/shard_map/all_to_all | solution.py:73
  52.3 6.3 %fusion.9 = f32[4,1,54,2048]{3,2,0,1:T(8,128)S(1)} fusion(bf16[4,54,3072]{2,1,0:T(8,128)(2,1)S(1)} %all_to_all.21, bf16[1,3072,2048]{2,1,0:T(8,128)(2,1)} %param.9), kind=kOutput, calls=%fused_computation.7 | convolution fusion | flops 2717908992 | bytes 15679488 | tf_op jit(solution)/shard_map/tlcd,ldf->tlcf/dot_general | solution.py:48
  58.6 7.9 %fusion.18 = bf16[4,1,54,2048]{3,2,0,1:T(8,128)(2,1)S(1)} fusion(bf16[4,54,3072]{2,1,0:T(8,128)(2,1)S(1)} %all_to_all.21, bf16[1,3072,2048]{2,1,0:T(8,128)(2,1)} %param.10, f32[4,1,54,2048]{3,2,0,1:T(8,128)S(1)} %fusion.9), kind=kOutput, calls=%fused_computation.11 | convolution fusion | flops 2720563200 | bytes 16564224 | tf_op jit(solution)/shard_map/tlcd,ldf->tlcf/dot_general | solution.py:51
  66.5 0.2 dot_general.46
  66.7 9.0 %fusion.6 = f32[3072,216]{0,1:T(8,128)} fusion(bf16[216,2048]{1,0:T(8,128)(2,1)S(1)} %dot_general.46, bf16[1,2048,3072]{2,1,0:T(8,128)(2,1)} %param.11), kind=kOutput, calls=%fused_computation.6 | convolution fusion | flops 2717908992 | bytes 16121856 | tf_op jit(solution)/shard_map/tlcf,lfd->dtlc/dot_general | solution.py:77
  75.7 50.2 %reduce-scatter.2.cloned.1.call-done = f32[768,216]{0,1:T(8,128)} async-done(((f32[3072,216]{0,1:T(8,128)}), f32[768,216]{0,1:T(8,128)}) %reduce-scatter.2.cloned.1.call-update) | async-done | bytes 663568 | tf_op jit(solution)/shard_map/reduce_scatter | solution.py:78
  126.0 1.1 convert_bitcast_fusion
  127.1 0.1 all_to_all.16
  127.2 9.4 %all_to_all.22 = bf16[4,54,768]{2,1,0:T(8,128)(2,1)S(1)} all-to-all(bf16[4,54,768]{2,1,0:T(8,128)(2,1)S(1)} %all_to_all.16), channel_id=1, replica_groups=mesh['rep'=2,'tp'=4,'ep'=4] {'ep'}, dimensions={0} | all-to-all | bytes 663552 | tf_op jit(solution)/shard_map/all_to_all | solution.py:86
  136.6 0.1 all_to_all.18
  136.7 1.0 convolution_convert_fusion
  (17 shorter events, 0.3 us)
Async XLA Ops:
  6.5 23.9 %copy-start = (bf16[96,768]{1,0:T(8,128)(2,1)S(1)}, bf16[96,768]{1,0:T(8,128)(2,1)}, u32[]{:S(2)}) copy-start(bf16[96,768]{1,0:T(8,128)(2,1)} %param.6) | copy-start | bytes 442372
  6.5 119.4 %reduce-scatter.2.cloned.1.call-start = ((), (), s32[]{:S(2)}) async-start(), calls=%async_computation.3 | async-start | bytes 3317760 | tf_op jit(solution)/shard_map/reduce_scatter | solution.py:78
  6.5 9.2 %collective-permute-start = (bf16[96,768]{1,0:T(8,128)(2,1)}, bf16[96,768]{1,0:T(8,128)(2,1)S(1)}, u32[]{:S(2)}, u32[]{:S(2)}) collective-permute-start(bf16[96,768]{1,0:T(8,128)(2,1)} %param.6), channel_id=1, source_target_pairs={{0,4},{4,8},{8,12},{12,0},{1,5},{5,9},{9,13},{13,1},{2,6},{6,10},{... | collective-permute-start | bytes 442376 | tf_op jit(solution)/shard_map/ppermute | solution.py:12
  15.7 6.9 %collective-permute-start.1 = (bf16[96,768]{1,0:T(8,128)(2,1)S(1)}, bf16[96,768]{1,0:T(8,128)(2,1)S(1)}, u32[]{:S(2)}, u32[]{:S(2)}) collective-permute-start(bf16[96,768]{1,0:T(8,128)(2,1)S(1)} %collective-permute-done), channel_id=1, source_target_pairs={{0,4},{4,8},{8,12},{12,0},{1,5},{5,9},{9,13},{13,1},{2,6},{6,10},{... | collective-permute-start | bytes 442376 | tf_op jit(solution)/shard_map/ppermute | solution.py:12
  22.7 6.9 %collective-permute-start.2 = (bf16[96,768]{1,0:T(8,128)(2,1)S(1)}, bf16[96,768]{1,0:T(8,128)(2,1)S(1)}, u32[]{:S(2)}, u32[]{:S(2)}) collective-permute-start(bf16[96,768]{1,0:T(8,128)(2,1)S(1)} %collective-permute-done.1), channel_id=1, source_target_pairs={{0,4},{4,8},{8,12},{12,0},{1,5},{5,9},{9,13},{13,1},{2,6},{6,10},{... | collective-permute-start | bytes 442376 | tf_op jit(solution)/shard_map/ppermute | solution.py:12
Sparse Core Ops, SparseCore 0:
  75.9 50.0 reduce-scatter.1
